TPU v7x, 32 devices: a whole 2x2x4 slice. The times are simulated.
32 devices in a mesh: cache: 8 (over z, y), group: 4 (over x, core).
Axes of the slice: x: 2, y: 2, z: 4, core: 2. Of those that a mesh axis runs over, the one named last changes fastest.
Arguments:
- queries: bfloat16 [32, 4096], P('cache'), may hold values from -240 to 240
- request_of: int32 [32], P('cache'), may hold values from 0 to 1, as said below
- selected: int32 [32, 8, 4], P('cache', 'group'), may hold values from 0 to 15, as said below
- cache_keys: bfloat16 [2, 8, 2048, 128], P(None, 'group', 'cache'), may hold values from -6 to 6
- cache_values: bfloat16 [2, 8, 2048, 128], P(None, 'group', 'cache'), may hold values from -6 to 6
- recent_keys: bfloat16 [32, 8, 1024, 128], P('cache', None, 'group'), may hold values from -6 to 6
- recent_values: bfloat16 [32, 8, 1024, 128], P('cache', None, 'group'), may hold values from -6 to 6
Outputs:
- attended: bfloat16 [32, 4096], P('cache', 'group')
Inputs may be any that keep to these rules, and one draw needn't show every extreme that they name: `request_of`: each prompt is read by exactly 16 slots. `selected`: for each slot and key-value head the 4 block ids have distinct owners id // 2; the 4 slots of one index of cache, with the key-value heads of one index of group, select at most 4 blocks held by any one owner, and exactly 4 from some owner.
All inputs are finite; a program needn't handle non-finite values.
Results may differ from a plain program's by a relative error of at most 0.0015.
Values may be sent and summed in bfloat16 or wider, within the bound.
No kernel may reach another device: no remote copies, remote signals or barrier semaphores. Data moves between devices by JAX's collectives and lax.ppermute only.
A program may use at most 64 MiB of HBM per device.

v0:
```python
import functools

import jax
import jax.numpy as jnp
from jax import lax
from jax.experimental import pallas as pl
from jax.experimental.pallas import tpu as pltpu
from jax.sharding import PartitionSpec as P


BLOCK = 128
LANES = 128
LOW = -1e30

ASK_FLOPS = 10**9
IN_VMEM = pl.BlockSpec(memory_space=pltpu.VMEM)
IN_HBM = pl.BlockSpec(memory_space=pl.ANY)


PARAMS = pltpu.CompilerParams(vmem_limit_bytes=16 * 1024 * 1024)


def stay(array):
    return pltpu.with_memory_space_constraint(array, pltpu.HBM)


def keep(array):
    return pltpu.with_memory_space_constraint(array, pltpu.VMEM)


def split_product(exponent, values_of, masks):
    rows = exponent.shape[0]
    high = exponent.astype(jnp.bfloat16).astype(jnp.float32)
    both = jnp.concatenate([high, exponent - high], axis=0)
    total = None
    for index, mask in enumerate(masks):
        part = jnp.where(jnp.concatenate([mask, mask], axis=0), both, 0.0).astype(jnp.bfloat16)
        term = jnp.dot(part, values_of(index), preferred_element_type=jnp.float32)
        total = term if total is None else total + term
    return total[:rows] + total[rows:]


def statistics(highest, totals, head, rows, lead):
    half_rows = rows // 2
    shape = (lead * rows, LANES)
    lane = lax.broadcasted_iota(jnp.int32, shape, 1)
    row = lax.broadcasted_iota(jnp.int32, shape, 0)
    place = 2 * head + (row % rows) // half_rows
    tile = jnp.where(lane == place, highest, 0.0) + jnp.where(
        lane == place + LANES // 2, totals, 0.0
    )
    tile = tile.reshape(lead, rows, LANES)
    return tile[:, :half_rows] + tile[:, half_rows:]


def ask_kernel(order, row_count, mine_heads, per_kv, top_count, per_owner, q_hbm, prompt_hbm, sel_hbm,
               out_ref, q_rows_ref, q_ref, prompt_ref, sel_ref, rows_ref, code_ref, sems):
    rows = row_count * per_kv
    pairs = ((q_hbm, q_ref), (prompt_hbm, prompt_ref), (sel_hbm, sel_ref))
    copies = [
        pltpu.make_async_copy(source, target, sems.at[index])
        for index, (source, target) in enumerate(pairs)
    ]
    for copy in copies:
        copy.start()
    code_ref[...] = jnp.full(code_ref.shape, -1.0, jnp.float32)
    for copy in copies:
        copy.wait()
    for tile in range(q_ref.shape[1] // LANES):
        head, query = divmod(tile, per_kv)
        rows_ref[pl.ds(head * rows + query, row_count, stride=per_kv), :] = q_ref[
            :, tile * LANES : (tile + 1) * LANES
        ].astype(jnp.float32)
    q_rows_ref[...] = rows_ref[...].astype(q_rows_ref.dtype)
    for head in range(mine_heads):
        for row in range(row_count):
            at = (head * row_count + row) * per_kv
            for top in range(top_count):
                block = sel_ref[row, head, top]
                owner = block // per_owner
                code = prompt_ref[row] * per_owner + block % per_owner
                code_ref[owner, at : at + per_kv, :] = jnp.full(
                    (per_kv, LANES), code, jnp.int32
                ).astype(jnp.float32)
    first = pl.multiple_of(lax.axis_index("group") * (mine_heads * rows), mine_heads * rows)
    mine = rows_ref[pl.ds(first, mine_heads * rows), :].astype(out_ref.dtype)
    for place, owner in enumerate(order):
        out_ref[place, :, :LANES] = mine
        out_ref[place, :, LANES:] = code_ref[owner].astype(out_ref.dtype)


def near_kernel(row_count, mine_heads, per_kv, scale, q_ref, k_ref, v_hbm, *rest):
    outs, (v_ref, scores_ref, summed_ref, stats_ref, sems) = rest[:-5], rest[-5:]
    group_count = len(outs)
    heads = group_count * mine_heads
    me = lax.axis_index("group")
    rows = per_kv * row_count
    half = rows // 2
    copies = []
    for index in range(group_count):
        at = pl.ds(index * mine_heads, mine_heads)
        copies.append(pltpu.make_async_copy(v_hbm.at[:, at], v_ref.at[:, at], sems.at[index]))
        copies[index].start()
    slot = lax.broadcasted_iota(jnp.int32, (rows, 1), 0) // per_kv
    for head in range(heads):
        q = q_ref[head * rows : (head + 1) * rows, :]
        scores = None
        for row in range(row_count):
            part = lax.dot_general(
                q, k_ref[row, head], (((1,), (1,)), ((), ())), preferred_element_type=jnp.float32
            )
            scores = part if scores is None else jnp.where(slot == row, part, scores)
        scores_ref[head * rows : (head + 1) * rows, :] = scores
    scores = scores_ref[...] * scale
    highest = jnp.max(scores, axis=1, keepdims=True)
    exponent = jnp.exp(scores - highest)
    totals = jnp.sum(exponent, axis=1, keepdims=True)
    high = exponent.astype(jnp.bfloat16)
    rest_part = (exponent - high.astype(jnp.float32)).astype(jnp.bfloat16)
    for head in range(heads):
        if head % mine_heads == 0:
            copies[head // mine_heads].wait()
        at = slice(head * rows, (head + 1) * rows)
        both = jnp.concatenate([high[at], rest_part[at]], axis=0)
        summed = None
        for row in range(row_count):
            part = jnp.dot(both, v_ref[row, head], preferred_element_type=jnp.float32)
            part = part[:rows] + part[rows:]
            summed = part if summed is None else jnp.where(slot == row, part, summed)
        summed_ref[at, :] = summed
        tile = statistics(highest[at], totals[at], head % mine_heads, rows, 1)[0]
        at = slice(head // mine_heads * half, (head // mine_heads + 1) * half)
        stats_ref[at, :] = tile if head % mine_heads == 0 else stats_ref[at, :] + tile
    count = mine_heads * rows
    for step in range(group_count):
        peer = partner(me, step, group_count)
        outs[step][:count, :] = summed_ref[pl.ds(pl.multiple_of(peer * count, count), count), :]
        outs[step][count:, :] = stats_ref[pl.ds(pl.multiple_of(peer * half, half), half), :]


def far_kernel(mine_heads, rows, per_owner, scale, ask_ref, k_ref, v_ref, out_ref):
    lead = ask_ref.shape[0]
    prompt_count = k_ref.shape[0]
    stats = None
    for head in range(mine_heads):
        mine = ask_ref[:, head * rows : (head + 1) * rows, :]
        q = mine[:, :, :LANES].reshape(lead * rows, LANES)
        code = mine[:, :, LANES:].reshape(lead * rows, LANES).astype(jnp.float32)
        scores = jnp.full(code.shape, LOW, jnp.float32)
        masks = []
        for prompt in range(prompt_count):
            part = lax.dot_general(
                q, k_ref[prompt, head], (((1,), (1,)), ((), ())),
                preferred_element_type=jnp.float32,
            )
            for block in range(per_owner):
                mask = code == float(prompt * per_owner + block)
                masks.append(mask)
                scores = jnp.where(
                    mask, part[:, block * BLOCK : (block + 1) * BLOCK] * scale, scores
                )
        highest = jnp.max(scores, axis=1, keepdims=True)
        exponent = jnp.where(code >= 0.0, jnp.exp(scores - highest), 0.0)
        totals = jnp.sum(exponent, axis=1, keepdims=True)

        def values_of(index):
            prompt, block = divmod(index, per_owner)
            return v_ref[prompt, head, block * BLOCK : (block + 1) * BLOCK, :]

        summed = split_product(exponent, values_of, masks)
        out_ref[:, head * rows : (head + 1) * rows, :] = summed.reshape(lead, rows, LANES)
        tile = statistics(highest, totals, head, rows, lead)
        stats = tile if stats is None else stats + tile
    out_ref[:, mine_heads * rows :, :] = stats


def gather_kernel(mine_heads, parts_ref, out_ref):
    count = parts_ref.shape[0]
    half = parts_ref.shape[1] // (2 * mine_heads + 1)
    rows = 2 * mine_heads * half
    stats = [parts_ref[index, rows:, :] for index in range(count)]
    lane = lax.broadcasted_iota(jnp.int32, stats[0].shape, 1)
    peak = functools.reduce(jnp.maximum, stats)
    factors = [jnp.exp(tile - peak) for tile in stats]
    weights = [factor * pltpu.roll(tile, LANES // 2, 1) for tile, factor in zip(stats, factors)]
    weight = functools.reduce(jnp.add, weights)
    for index in range(2 * mine_heads):
        at = slice(index * half, (index + 1) * half)
        terms = [
            factor[:, index : index + 1] * parts_ref[part, at, :]
            for part, factor in enumerate(factors)
        ]
        out_ref[at, :] = functools.reduce(jnp.add, terms)
    out_ref[rows:, :] = jnp.where(lane < LANES // 2, peak, pltpu.roll(weight, LANES // 2, 1))


def merge_kernel(row_count, mine_heads, per_kv, *rest):
    near_refs, out_ref, rows_ref = rest[:-2], rest[-2], rest[-1]
    rows = per_kv * row_count
    half = rows // 2
    count = mine_heads * rows
    stats = [ref[count:, :] for ref in near_refs]
    peak = functools.reduce(jnp.maximum, stats)
    factors = [jnp.exp(tile - peak) for tile in stats]
    weight = None
    for tile, factor in zip(stats, factors):
        term = factor * pltpu.roll(tile, LANES // 2, 1)
        weight = term if weight is None else weight + term
    lane = lax.broadcasted_iota(jnp.int32, weight.shape, 1)
    weight = jnp.where(lane < 2 * mine_heads, weight, 1.0)
    factors = [factor / weight for factor in factors]
    for index in range(2 * mine_heads):
        at = slice(index * half, (index + 1) * half)
        total = None
        for ref, factor in zip(near_refs, factors):
            term = factor[:, index : index + 1] * ref[at, :]
            total = term if total is None else total + term
        rows_ref[at, :] = total
    for head in range(mine_heads):
        for query in range(per_kv):
            tile = head * per_kv + query
            out_ref[:, tile * LANES : (tile + 1) * LANES] = rows_ref[
                pl.ds(head * rows + query, row_count, stride=per_kv), :
            ].astype(out_ref.dtype)


def middle_first(count):
    middle = list(range(count))[count // 2 : count // 2 + 2]
    return middle + [owner for owner in range(count) if owner not in middle]


def exchange(array, order):
    return lax.all_to_all(
        array, "cache", split_axis=0, concat_axis=0, tiled=True, axis_index_groups=[order]
    )


def partner(me, step, count):
    if count & (count - 1) == 0:
        return me ^ step
    return lax.rem(me + step, count)


def work(queries, request_of, selected, cache_keys, cache_values, recent_keys, recent_values):
    row_count = queries.shape[0]
    heads_kv = recent_keys.shape[1]
    near_tokens = recent_keys.shape[2]
    head_dim = recent_keys.shape[3]
    per_kv = queries.shape[1] // (heads_kv * head_dim)
    mine_heads = selected.shape[1]
    top_count = selected.shape[2]
    score_scale = head_dim ** (-0.5)
    owner_count = lax.axis_size("cache")
    group_count = lax.axis_size("group")
    held = cache_keys.shape[2]
    per_owner = held // BLOCK
    order = middle_first(owner_count)
    rows = per_kv * row_count
    count = mine_heads * rows
    packed = count + rows // 2

    ask, query_rows = pl.pallas_call(
        functools.partial(ask_kernel, order, row_count, mine_heads, per_kv, top_count, per_owner),
        compiler_params=PARAMS,
        cost_estimate=pl.CostEstimate(flops=ASK_FLOPS, bytes_accessed=1 << 20, transcendentals=0),
        out_shape=[
            jax.ShapeDtypeStruct((owner_count, count, 2 * head_dim), queries.dtype),
            pltpu.VMEM((heads_kv * rows, head_dim), queries.dtype),
        ],
        in_specs=[IN_HBM] * 3,
        out_specs=[IN_VMEM] * 2,
        scratch_shapes=[
            pltpu.VMEM(queries.shape, queries.dtype),
            pltpu.SMEM(request_of.shape, request_of.dtype),
            pltpu.SMEM(selected.shape, selected.dtype),
            pltpu.VMEM((heads_kv * rows, head_dim), jnp.float32),
            pltpu.VMEM((owner_count, count, head_dim), jnp.float32),
            pltpu.SemaphoreType.DMA((3,)),
        ],
    )(stay(queries), stay(request_of), stay(selected))
    asked = exchange(ask, order)

    near = pl.pallas_call(
        functools.partial(near_kernel, row_count, mine_heads, per_kv, score_scale),
        compiler_params=PARAMS,
        out_shape=[pltpu.VMEM((packed, head_dim), jnp.float32)] * group_count,
        in_specs=[IN_VMEM, IN_VMEM, IN_HBM],
        out_specs=[IN_VMEM] * group_count,
        scratch_shapes=[
            pltpu.VMEM(recent_values.shape, recent_values.dtype),
            pltpu.VMEM((heads_kv * rows, near_tokens), jnp.float32),
            pltpu.VMEM((heads_kv * rows, head_dim), jnp.float32),
            pltpu.VMEM((group_count * rows // 2, head_dim), jnp.float32),
            pltpu.SemaphoreType.DMA((group_count,)),
        ],
    )(keep(query_rows), keep(recent_keys), stay(recent_values))
    own = near[0]
    asked, own = lax.optimization_barrier((asked, own))
    parts = [own]
    for step in range(1, group_count):
        parts.append(lax.ppermute(near[step], "group", [(i, i ^ step) for i in range(group_count)]))
    near = parts

    lead = min(owner_count, 8)
    if owner_count == lead:
        specs = dict(
            in_specs=[IN_VMEM] * 3,
            out_specs=IN_VMEM,
            out_shape=pltpu.VMEM((owner_count, packed, head_dim), jnp.float32),
        )
        asked = keep(asked)
    else:
        specs = dict(
            grid=(owner_count // lead,),
            in_specs=[pl.BlockSpec((lead, count, 2 * head_dim), lambda i: (i, 0, 0)), IN_VMEM, IN_VMEM],
            out_specs=pl.BlockSpec((lead, packed, head_dim), lambda i: (i, 0, 0)),
            out_shape=jax.ShapeDtypeStruct((owner_count, packed, head_dim), jnp.float32),
        )
    far = pl.pallas_call(
        functools.partial(far_kernel, mine_heads, rows, per_owner, score_scale), compiler_params=PARAMS, **specs
    )(asked, keep(cache_keys), keep(cache_values))

    far = exchange(far, order)
    far = pl.pallas_call(
        functools.partial(gather_kernel, mine_heads), compiler_params=PARAMS,
        out_shape=pltpu.VMEM((packed, head_dim), jnp.float32),
        in_specs=[IN_VMEM],
        out_specs=IN_VMEM,
    )(keep(far))

    return pl.pallas_call(
        functools.partial(merge_kernel, row_count, mine_heads, per_kv), compiler_params=PARAMS,
        out_shape=jax.ShapeDtypeStruct((row_count, count // row_count * head_dim), jnp.bfloat16),
        in_specs=[IN_VMEM] * (1 + group_count),
        out_specs=IN_VMEM,
        scratch_shapes=[pltpu.VMEM((count, head_dim), jnp.float32)],
    )(*[keep(part) for part in (far, *near)])


def solution(mesh):
    return jax.shard_map(
        work,
        mesh=mesh,
        in_specs=(
            P("cache", None),
            P("cache"),
            P("cache", "group", None),
            P(None, "group", "cache", None),
            P(None, "group", "cache", None),
            P("cache", None, "group", None),
            P("cache", None, "group", None),
        ),
        out_specs=P("cache", "group"),
        check_vma=False,
    )
```

profile of v0, /device:TPU:0, one launch (start us, length us, event | category | flops | bytes accessed | tf_op | source)
XLA Modules:
  0.0 26.0 jit_solution(13499316406423218523)
XLA Ops:
  0.0 0.0 copy-start
  0.0 1.8 %shard_map.73 = (bf16[8,32,256]{2,1,0:T(8,128)(2,1)}, bf16[128,128]{1,0:T(8,128)(2,1)S(1)}) custom-call(bf16[4,4096]{1,0:T(4,128)(2,1)} %q_hbm.1, s32[4]{0:T(128)} %prompt_hbm.1, s32[4,2,4]{2,1,0:T(2,128)} %sel_hbm.1), custom_call_target="tpu_custom_call" | custom-call | flops 1000000000 | bytes 1048576 | tf_op jit(solution)/shard_map/pallas_call | solution.py:262
  1.8 7.9 %all-to-all-start = ((bf16[8,32,256]{2,1,0:T(8,128)(2,1)}), bf16[8,32,256]{2,1,0:T(8,128)(2,1)S(1)}, u32[]{:S(2)}, u32[]{:S(2)}) async-start(bf16[8,32,256]{2,1,0:T(8,128)(2,1)} %get-tuple-element.13), calls=%async_computation | async-start | bytes 262144 | tf_op jit(solution)/shard_map/all_to_all | solution.py:233
  9.7 0.0 copy-done
  9.7 0.0 copy-start.1
  9.7 0.0 copy-start.2
  9.7 2.0 %shard_map.74 = (f32[40,128]{1,0:T(8,128)S(1)}, f32[40,128]{1,0:T(8,128)S(1)}, f32[40,128]{1,0:T(8,128)S(1)}, f32[40,128]{1,0:T(8,128)S(1)}) custom-call(bf16[128,128]{1,0:T(8,128)(2,1)S(1)} %get-tuple-element.14.q_ref, bf16[4,8,256,128]{3,2,1,0:T(8,128)(2,1)S(1)} %copy-done, bf16[4,8,256,128]{3,2,1,0:T(8,128)(2,1)} %v_hbm.1), custom_call_target="tpu_custom_call" | custom-call | tf_op jit(solution)/shard_map/pallas_call | solution.py:283
  11.8 2.2 %all-to-all-done.ask_ref = bf16[8,32,256]{2,1,0:T(8,128)(2,1)S(1)} async-done(((bf16[8,32,256]{2,1,0:T(8,128)(2,1)}), bf16[8,32,256]{2,1,0:T(8,128)(2,1)S(1)}, u32[]{:S(2)}, u32[]{:S(2)}) %all-to-all-start) | async-done | bytes 131104 | tf_op jit(solution)/shard_map/all_to_all | solution.py:233
  14.0 0.0 copy-done.1
  14.0 0.0 copy-done.2
  14.0 1.2 %shard_map.75 = f32[8,40,128]{2,1,0:T(8,128)} custom-call(bf16[8,32,256]{2,1,0:T(8,128)(2,1)S(1)} %all-to-all-done.ask_ref, bf16[2,2,256,128]{3,2,1,0:T(8,128)(2,1)S(1)} %copy-done.1, bf16[2,2,256,128]{3,2,1,0:T(8,128)(2,1)S(1)} %copy-done.2), custom_call_target="tpu_custom_call" | custom-call | tf_op jit(solution)/shard_map/pallas_call | solution.py:319
  15.2 5.3 %all-to-all-start.1 = ((f32[8,40,128]{2,1,0:T(8,128)}), f32[8,40,128]{2,1,0:T(8,128)S(1)}, u32[]{:S(2)}, u32[]{:S(2)}) async-start(f32[8,40,128]{2,1,0:T(8,128)} %shard_map.75), calls=%async_computation.1 | async-start | bytes 327680 | tf_op jit(solution)/shard_map/all_to_all | solution.py:233
  20.5 0.0 collective-permute-start
  20.5 1.5 %collective-permute-start.1 = (f32[40,128]{1,0:T(8,128)S(1)}, f32[40,128]{1,0:T(8,128)S(1)}, u32[]{:S(2)}, u32[]{:S(2)}) collective-permute-start(f32[40,128]{1,0:T(8,128)S(1)} %get-tuple-element.19), channel_id=1, source_target_pairs={{0,2},{1,3},{2,0},{3,1},{4,6},{5,7},{6,4},{7,5},{8,10},{9,11},{10,... | collective-permute-start | bytes 61448 | tf_op jit(solution)/shard_map/ppermute | solution.py:301
  22.0 0.4 %collective-permute-start.2 = (f32[40,128]{1,0:T(8,128)S(1)}, f32[40,128]{1,0:T(8,128)S(1)}, u32[]{:S(2)}, u32[]{:S(2)}) collective-permute-start(f32[40,128]{1,0:T(8,128)S(1)} %get-tuple-element.20), channel_id=1, source_target_pairs={{0,3},{1,2},{2,1},{3,0},{4,7},{5,6},{6,5},{7,4},{8,11},{9,10},{10,... | collective-permute-start | bytes 61448 | tf_op jit(solution)/shard_map/ppermute | solution.py:301
  22.4 2.7 %all-to-all-done.1.parts_ref = f32[8,40,128]{2,1,0:T(8,128)S(1)} async-done(((f32[8,40,128]{2,1,0:T(8,128)}), f32[8,40,128]{2,1,0:T(8,128)S(1)}, u32[]{:S(2)}, u32[]{:S(2)}) %all-to-all-start.1) | async-done | bytes 163872 | tf_op jit(solution)/shard_map/all_to_all | solution.py:233
  25.1 0.1 shard_map.76.rest_0_
  25.2 0.0 collective-permute-done.rest_2_
  25.2 0.0 collective-permute-done.1.rest_3_
  25.2 0.0 collective-permute-done.2.rest_4_
  25.2 0.8 %shard_map.77 = bf16[4,1024]{1,0:T(4,128)(2,1)} custom-call(f32[40,128]{1,0:T(8,128)S(1)} %shard_map.76.rest_0_, f32[40,128]{1,0:T(8,128)S(1)} %get-tuple-element.17.rest_1_, f32[40,128]{1,0:T(8,128)S(1)} %collective-permute-done.rest_2_, f32[40,128]{1,0:T(8,128)S(1)} %collective-permute-done.1.rest_3_, f32[40,128]{1,0:T(8,128)S(1)} %collective-permute-done.2.rest_4_), custom_call_target="tpu_custom_call" | custom-call | tf_op jit(solution)/shard_map/pallas_call | solution.py:331
Async XLA Ops:
  0.0 9.7 %copy-start = (bf16[4,8,256,128]{3,2,1,0:T(8,128)(2,1)S(1)}, bf16[4,8,256,128]{3,2,1,0:T(8,128)(2,1)}, u32[]{:S(2)}) copy-start(bf16[4,8,256,128]{3,2,1,0:T(8,128)(2,1)} %k_ref.2) | copy-start | bytes 6291460
  1.8 12.2 %all-to-all-start = ((bf16[8,32,256]{2,1,0:T(8,128)(2,1)}), bf16[8,32,256]{2,1,0:T(8,128)(2,1)S(1)}, u32[]{:S(2)}, u32[]{:S(2)}) async-start(bf16[8,32,256]{2,1,0:T(8,128)(2,1)} %get-tuple-element.13), calls=%async_computation | async-start | bytes 262144 | tf_op jit(solution)/shard_map/all_to_all | solution.py:233
  9.7 4.3 %copy-start.1 = (bf16[2,2,256,128]{3,2,1,0:T(8,128)(2,1)S(1)}, bf16[2,2,256,128]{3,2,1,0:T(8,128)(2,1)}, u32[]{:S(2)}) copy-start(bf16[2,2,256,128]{3,2,1,0:T(8,128)(2,1)} %k_ref.3) | copy-start | bytes 786436
  9.7 4.3 %copy-start.2 = (bf16[2,2,256,128]{3,2,1,0:T(8,128)(2,1)S(1)}, bf16[2,2,256,128]{3,2,1,0:T(8,128)(2,1)}, u32[]{:S(2)}) copy-start(bf16[2,2,256,128]{3,2,1,0:T(8,128)(2,1)} %v_ref.1) | copy-start | bytes 786436
  15.2 9.8 %all-to-all-start.1 = ((f32[8,40,128]{2,1,0:T(8,128)}), f32[8,40,128]{2,1,0:T(8,128)S(1)}, u32[]{:S(2)}, u32[]{:S(2)}) async-start(f32[8,40,128]{2,1,0:T(8,128)} %shard_map.75), calls=%async_computation.1 | async-start | bytes 327680 | tf_op jit(solution)/shard_map/all_to_all | solution.py:233
  20.5 4.7 %collective-permute-start = (f32[40,128]{1,0:T(8,128)S(1)}, f32[40,128]{1,0:T(8,128)S(1)}, u32[]{:S(2)}, u32[]{:S(2)}) collective-permute-start(f32[40,128]{1,0:T(8,128)S(1)} %get-tuple-element.18), channel_id=1, source_target_pairs={{0,1},{1,0},{2,3},{3,2},{4,5},{5,4},{6,7},{7,6},{8,9},{9,8},{10,11... | collective-permute-start | bytes 61448 | tf_op jit(solution)/shard_map/ppermute | solution.py:301
  20.5 4.7 %collective-permute-start.1 = (f32[40,128]{1,0:T(8,128)S(1)}, f32[40,128]{1,0:T(8,128)S(1)}, u32[]{:S(2)}, u32[]{:S(2)}) collective-permute-start(f32[40,128]{1,0:T(8,128)S(1)} %get-tuple-element.19), channel_id=1, source_target_pairs={{0,2},{1,3},{2,0},{3,1},{4,6},{5,7},{6,4},{7,5},{8,10},{9,11},{10,... | collective-permute-start | bytes 61448 | tf_op jit(solution)/shard_map/ppermute | solution.py:301
  22.0 3.2 %collective-permute-start.2 = (f32[40,128]{1,0:T(8,128)S(1)}, f32[40,128]{1,0:T(8,128)S(1)}, u32[]{:S(2)}, u32[]{:S(2)}) collective-permute-start(f32[40,128]{1,0:T(8,128)S(1)} %get-tuple-element.20), channel_id=1, source_target_pairs={{0,3},{1,2},{2,1},{3,0},{4,7},{5,6},{6,5},{7,4},{8,11},{9,10},{10,... | collective-permute-start | bytes 61448 | tf_op jit(solution)/shard_map/ppermute | solution.py:301
where the time goes:
time: 26.4 us; the launch traced here: 26 us
  starting transfers between devices  15 us (57%)
  Pallas kernels  6.02 us (23%)
  waiting for transfers between devices  4.94 us (19%)
    all_to_all x2, starting transfers between devices, exchange(): lax.all_to_all(array, 'cache', split_axis=0, concat_axis=0, tiled=True, a...  13.2 us
    all_to_all x2, waiting for transfers between devices, exchange(): lax.all_to_all(array, 'cache', split_axis=0, concat_axis=0, tiled=True, a...  4.93 us
    pallas_call x1, Pallas kernels, work(): pl.pallas_call(functools.partial(near_kernel, row_count, mine_heads, per_...  2.03 us
    ppermute x3, starting transfers between devices, work(): lax.ppermute(near[step], 'group', [(i, i ^ step) for i in range(group_cou...  1.86 us
    pallas_call x1, Pallas kernels, work(): pl.pallas_call(functools.partial(ask_kernel, order, row_count, mine_heads...  1.82 us
    pallas_call x1, Pallas kernels, work(): pl.pallas_call(functools.partial(far_kernel, mine_heads, rows, per_owner,...  1.24 us
    pallas_call x1, Pallas kernels, work(): pl.pallas_call(functools.partial(merge_kernel, row_count, mine_heads, per...  0.79 us
  transfers between devices with their start and end apart: 5, of which 2 were waited for; matrix products, arithmetic and copies ran while one was open for 0% of the time, Pallas kernels for 8%

commit v1 on v0

--- a/solution.py
+++ b/solution.py
@@ -54,8 +54,8 @@
 
 
 def ask_kernel(order, row_count, mine_heads, per_kv, top_count, per_owner, q_hbm, prompt_hbm, sel_hbm,
-               out_ref, q_rows_ref, q_ref, prompt_ref, sel_ref, rows_ref, code_ref, sems):
-    rows = row_count * per_kv
+               out_hbm, q_ref, prompt_ref, sel_ref, rows_ref, mine_ref, code_ref, codes_ref, sems):
+    first = lax.axis_index("group") * (mine_heads * per_kv)
     pairs = ((q_hbm, q_ref), (prompt_hbm, prompt_ref), (sel_hbm, sel_ref))
     copies = [
         pltpu.make_async_copy(source, target, sems.at[index])
@@ -64,33 +64,44 @@
     for copy in copies:
         copy.start()
     code_ref[...] = jnp.full(code_ref.shape, -1.0, jnp.float32)
-    for copy in copies:
+    copies[0].wait()
+    for head in range(mine_heads):
+        for query in range(per_kv):
+            start = pl.multiple_of((first + head * per_kv + query) * LANES, LANES)
+            at = head * row_count * per_kv + query
+            rows_ref[pl.ds(at, row_count, stride=per_kv), :] = q_ref[
+                :, pl.ds(start, LANES)
+            ].astype(jnp.float32)
+    mine_ref[...] = rows_ref[...].astype(mine_ref.dtype)
+    sends = [
+        pltpu.make_async_copy(mine_ref, out_hbm.at[place, :, :LANES], sems.at[3 + place])
+        for place in range(len(order))
+    ]
+    for copy in sends:
+        copy.start()
+    for copy in copies[1:]:
         copy.wait()
-    for tile in range(q_ref.shape[1] // LANES):
-        head, query = divmod(tile, per_kv)
-        rows_ref[pl.ds(head * rows + query, row_count, stride=per_kv), :] = q_ref[
-            :, tile * LANES : (tile + 1) * LANES
-        ].astype(jnp.float32)
-    q_rows_ref[...] = rows_ref[...].astype(q_rows_ref.dtype)
     for head in range(mine_heads):
         for row in range(row_count):
             at = (head * row_count + row) * per_kv
             for top in range(top_count):
                 block = sel_ref[row, head, top]
-                owner = block // per_owner
-                code = prompt_ref[row] * per_owner + block % per_owner
+                owner = lax.div(block, per_owner)
+                code = prompt_ref[row] * per_owner + lax.rem(block, per_owner)
                 code_ref[owner, at : at + per_kv, :] = jnp.full(
                     (per_kv, LANES), code, jnp.int32
                 ).astype(jnp.float32)
-    first = pl.multiple_of(lax.axis_index("group") * (mine_heads * rows), mine_heads * rows)
-    mine = rows_ref[pl.ds(first, mine_heads * rows), :].astype(out_ref.dtype)
     for place, owner in enumerate(order):
-        out_ref[place, :, :LANES] = mine
-        out_ref[place, :, LANES:] = code_ref[owner].astype(out_ref.dtype)
-
-
-def near_kernel(row_count, mine_heads, per_kv, scale, q_ref, k_ref, v_hbm, *rest):
-    outs, (v_ref, scores_ref, summed_ref, stats_ref, sems) = rest[:-5], rest[-5:]
+        codes_ref[place] = code_ref[owner].astype(codes_ref.dtype)
+    last = pltpu.make_async_copy(codes_ref, out_hbm.at[:, :, LANES:], sems.at[3 + len(order)])
+    last.start()
+    for copy in sends:
+        copy.wait()
+    last.wait()
+
+
+def near_kernel(row_count, mine_heads, per_kv, scale, queries_ref, k_ref, v_hbm, *rest):
+    outs, (v_ref, q_ref, scores_ref, summed_ref, stats_ref, sems) = rest[:-6], rest[-6:]
     group_count = len(outs)
     heads = group_count * mine_heads
     me = lax.axis_index("group")
@@ -101,9 +112,14 @@
         at = pl.ds(index * mine_heads, mine_heads)
         copies.append(pltpu.make_async_copy(v_hbm.at[:, at], v_ref.at[:, at], sems.at[index]))
         copies[index].start()
+    for tile in range(heads * per_kv):
+        head, query = divmod(tile, per_kv)
+        q_ref[pl.ds(head * rows + query, row_count, stride=per_kv), :] = queries_ref[
+            :, tile * LANES : (tile + 1) * LANES
+        ].astype(jnp.float32)
     slot = lax.broadcasted_iota(jnp.int32, (rows, 1), 0) // per_kv
     for head in range(heads):
-        q = q_ref[head * rows : (head + 1) * rows, :]
+        q = q_ref[head * rows : (head + 1) * rows, :].astype(queries_ref.dtype)
         scores = None
         for row in range(row_count):
             part = lax.dot_general(
@@ -225,8 +241,12 @@
 
 
 def middle_first(count):
-    middle = list(range(count))[count // 2 : count // 2 + 2]
-    return middle + [owner for owner in range(count) if owner not in middle]
+    middle = count // 2
+    order = [middle]
+    for owner in [1, 0, middle + 1, middle - 1, middle - 2, *range(count)]:
+        if 0 <= owner < count and owner not in order:
+            order.append(owner)
+    return order
 
 
 def exchange(array, order):
@@ -259,23 +279,22 @@
     count = mine_heads * rows
     packed = count + rows // 2
 
-    ask, query_rows = pl.pallas_call(
+    ask = pl.pallas_call(
         functools.partial(ask_kernel, order, row_count, mine_heads, per_kv, top_count, per_owner),
         compiler_params=PARAMS,
         cost_estimate=pl.CostEstimate(flops=ASK_FLOPS, bytes_accessed=1 << 20, transcendentals=0),
-        out_shape=[
-            jax.ShapeDtypeStruct((owner_count, count, 2 * head_dim), queries.dtype),
-            pltpu.VMEM((heads_kv * rows, head_dim), queries.dtype),
-        ],
+        out_shape=jax.ShapeDtypeStruct((owner_count, count, 2 * head_dim), queries.dtype),
         in_specs=[IN_HBM] * 3,
-        out_specs=[IN_VMEM] * 2,
+        out_specs=IN_HBM,
         scratch_shapes=[
             pltpu.VMEM(queries.shape, queries.dtype),
             pltpu.SMEM(request_of.shape, request_of.dtype),
             pltpu.SMEM(selected.shape, selected.dtype),
-            pltpu.VMEM((heads_kv * rows, head_dim), jnp.float32),
+            pltpu.VMEM((count, head_dim), jnp.float32),
+            pltpu.VMEM((count, head_dim), queries.dtype),
             pltpu.VMEM((owner_count, count, head_dim), jnp.float32),
-            pltpu.SemaphoreType.DMA((3,)),
+            pltpu.VMEM((owner_count, count, head_dim), queries.dtype),
+            pltpu.SemaphoreType.DMA((4 + owner_count,)),
         ],
     )(stay(queries), stay(request_of), stay(selected))
     asked = exchange(ask, order)
@@ -288,12 +307,13 @@
         out_specs=[IN_VMEM] * group_count,
         scratch_shapes=[
             pltpu.VMEM(recent_values.shape, recent_values.dtype),
+            pltpu.VMEM((heads_kv * rows, head_dim), jnp.float32),
             pltpu.VMEM((heads_kv * rows, near_tokens), jnp.float32),
             pltpu.VMEM((heads_kv * rows, head_dim), jnp.float32),
             pltpu.VMEM((group_count * rows // 2, head_dim), jnp.float32),
             pltpu.SemaphoreType.DMA((group_count,)),
         ],
-    )(keep(query_rows), keep(recent_keys), stay(recent_values))
+    )(keep(queries), keep(recent_keys), stay(recent_values))
     own = near[0]
     asked, own = lax.optimization_barrier((asked, own))
     parts = [own]

time: 26.4 us -> 26 us (0.985)
  starting transfers between devices: 15 us -> 14.7 us
    all_to_all x2, starting transfers between devices: 13.2 us -> 12.8 us  [exchange(): lax.all_to_all(array, 'cache', split_axis=0, concat_axis=0, tiled=True, a...]
where the time goes in v1:
time: 26 us; the launch traced here: 25.6 us
  starting transfers between devices  14.7 us (57%)
  Pallas kernels  5.98 us (23%)
  waiting for transfers between devices  4.93 us (19%)
    all_to_all x2, starting transfers between devices, exchange(): lax.all_to_all(array, 'cache', split_axis=0, concat_axis=0, tiled=True, a...  12.8 us
    all_to_all x2, waiting for transfers between devices, exchange(): lax.all_to_all(array, 'cache', split_axis=0, concat_axis=0, tiled=True, a...  4.92 us
    pallas_call x1, Pallas kernels, work(): pl.pallas_call(functools.partial(near_kernel, row_count, mine_heads, per_...  2.01 us
    ppermute x3, starting transfers between devices, work(): lax.ppermute(near[step], 'group', [(i, i ^ step) for i in range(group_cou...  1.86 us
    pallas_call x1, Pallas kernels, work(): pl.pallas_call(functools.partial(ask_kernel, order, row_count, mine_heads...  1.79 us
    pallas_call x1, Pallas kernels, work(): pl.pallas_call(functools.partial(far_kernel, mine_heads, rows, per_owner,...  1.24 us
    pallas_call x1, Pallas kernels, work(): pl.pallas_call(functools.partial(merge_kernel, row_count, mine_heads, per...  0.79 us
  transfers between devices with their start and end apart: 5, of which 2 were waited for; matrix products, arithmetic and copies ran while one was open for 0% of the time, Pallas kernels for 8%

profile of v1, /device:TPU:0, one launch (start us, length us, event | category | flops | bytes accessed | tf_op | source)
XLA Modules:
  0.0 25.6 jit_solution(4460465270318619879)
XLA Ops:
  0.0 0.0 copy-start.3
  0.0 0.0 copy-start
  0.0 1.8 %shard_map.73 = bf16[8,32,256]{2,1,0:T(8,128)(2,1)} custom-call(bf16[4,4096]{1,0:T(4,128)(2,1)} %queries_ref.1, s32[4]{0:T(128)} %prompt_hbm.1, s32[4,2,4]{2,1,0:T(2,128)} %sel_hbm.1), custom_call_target="tpu_custom_call" | custom-call | flops 1000000000 | bytes 1048576 | tf_op jit(solution)/shard_map/pallas_call | solution.py:282
  1.8 7.9 %all-to-all-start = ((bf16[8,32,256]{2,1,0:T(8,128)(2,1)}), bf16[8,32,256]{2,1,0:T(8,128)(2,1)S(1)}, u32[]{:S(2)}, u32[]{:S(2)}) async-start(bf16[8,32,256]{2,1,0:T(8,128)(2,1)} %shard_map.73), calls=%async_computation | async-start | bytes 262144 | tf_op jit(solution)/shard_map/all_to_all | solution.py:253
  9.7 0.0 copy-done.3
  9.7 0.0 copy-done
  9.7 0.0 copy-start.1
  9.7 0.0 copy-start.2
  9.7 2.0 %shard_map.74 = (f32[40,128]{1,0:T(8,128)S(1)}, f32[40,128]{1,0:T(8,128)S(1)}, f32[40,128]{1,0:T(8,128)S(1)}, f32[40,128]{1,0:T(8,128)S(1)}) custom-call(bf16[4,4096]{1,0:T(4,128)(2,1)S(1)} %copy-done.3, bf16[4,8,256,128]{3,2,1,0:T(8,128)(2,1)S(1)} %copy-done, bf16[4,8,256,128]{3,2,1,0:T(8,128)(2,1)} %v_hbm.1), custom_call_target="tpu_custom_call" | custom-call | tf_op jit(solution)/shard_map/pallas_call | solution.py:302
  11.7 2.2 %all-to-all-done.ask_ref = bf16[8,32,256]{2,1,0:T(8,128)(2,1)S(1)} async-done(((bf16[8,32,256]{2,1,0:T(8,128)(2,1)}), bf16[8,32,256]{2,1,0:T(8,128)(2,1)S(1)}, u32[]{:S(2)}, u32[]{:S(2)}) %all-to-all-start) | async-done | bytes 131104 | tf_op jit(solution)/shard_map/all_to_all | solution.py:253
  14.0 0.0 copy-done.1
  14.0 0.0 copy-done.2
  14.0 1.2 %shard_map.75 = f32[8,40,128]{2,1,0:T(8,128)} custom-call(bf16[8,32,256]{2,1,0:T(8,128)(2,1)S(1)} %all-to-all-done.ask_ref, bf16[2,2,256,128]{3,2,1,0:T(8,128)(2,1)S(1)} %copy-done.1, bf16[2,2,256,128]{3,2,1,0:T(8,128)(2,1)S(1)} %copy-done.2), custom_call_target="tpu_custom_call" | custom-call | tf_op jit(solution)/shard_map/pallas_call | solution.py:339
  15.2 4.9 %all-to-all-start.1 = ((f32[8,40,128]{2,1,0:T(8,128)}), f32[8,40,128]{2,1,0:T(8,128)S(1)}, u32[]{:S(2)}, u32[]{:S(2)}) async-start(f32[8,40,128]{2,1,0:T(8,128)} %shard_map.75), calls=%async_computation.1 | async-start | bytes 327680 | tf_op jit(solution)/shard_map/all_to_all | solution.py:253
  20.1 0.0 collective-permute-start
  20.1 1.5 %collective-permute-start.1 = (f32[40,128]{1,0:T(8,128)S(1)}, f32[40,128]{1,0:T(8,128)S(1)}, u32[]{:S(2)}, u32[]{:S(2)}) collective-permute-start(f32[40,128]{1,0:T(8,128)S(1)} %get-tuple-element.15), channel_id=1, source_target_pairs={{0,2},{1,3},{2,0},{3,1},{4,6},{5,7},{6,4},{7,5},{8,10},{9,11},{10,... | collective-permute-start | bytes 61448 | tf_op jit(solution)/shard_map/ppermute | solution.py:321
  21.6 0.4 %collective-permute-start.2 = (f32[40,128]{1,0:T(8,128)S(1)}, f32[40,128]{1,0:T(8,128)S(1)}, u32[]{:S(2)}, u32[]{:S(2)}) collective-permute-start(f32[40,128]{1,0:T(8,128)S(1)} %get-tuple-element.16), channel_id=1, source_target_pairs={{0,3},{1,2},{2,1},{3,0},{4,7},{5,6},{6,5},{7,4},{8,11},{9,10},{10,... | collective-permute-start | bytes 61448 | tf_op jit(solution)/shard_map/ppermute | solution.py:321
  22.0 2.7 %all-to-all-done.1.parts_ref = f32[8,40,128]{2,1,0:T(8,128)S(1)} async-done(((f32[8,40,128]{2,1,0:T(8,128)}), f32[8,40,128]{2,1,0:T(8,128)S(1)}, u32[]{:S(2)}, u32[]{:S(2)}) %all-to-all-start.1) | async-done | bytes 163872 | tf_op jit(solution)/shard_map/all_to_all | solution.py:253
  24.7 0.1 shard_map.76.rest_0_
  24.8 0.0 collective-permute-done.rest_2_
  24.8 0.0 collective-permute-done.1.rest_3_
  24.8 0.0 collective-permute-done.2.rest_4_
  24.8 0.8 %shard_map.77 = bf16[4,1024]{1,0:T(4,128)(2,1)} custom-call(f32[40,128]{1,0:T(8,128)S(1)} %shard_map.76.rest_0_, f32[40,128]{1,0:T(8,128)S(1)} %get-tuple-element.13.rest_1_, f32[40,128]{1,0:T(8,128)S(1)} %collective-permute-done.rest_2_, f32[40,128]{1,0:T(8,128)S(1)} %collective-permute-done.1.rest_3_, f32[40,128]{1,0:T(8,128)S(1)} %collective-permute-done.2.rest_4_), custom_call_target="tpu_custom_call" | custom-call | tf_op jit(solution)/shard_map/pallas_call | solution.py:351
Async XLA Ops:
  0.0 9.7 %copy-start.3 = (bf16[4,4096]{1,0:T(4,128)(2,1)S(1)}, bf16[4,4096]{1,0:T(4,128)(2,1)}, u32[]{:S(2)}) copy-start(bf16[4,4096]{1,0:T(4,128)(2,1)} %queries_ref.1) | copy-start | bytes 98308
  0.0 9.7 %copy-start = (bf16[4,8,256,128]{3,2,1,0:T(8,128)(2,1)S(1)}, bf16[4,8,256,128]{3,2,1,0:T(8,128)(2,1)}, u32[]{:S(2)}) copy-start(bf16[4,8,256,128]{3,2,1,0:T(8,128)(2,1)} %k_ref.2) | copy-start | bytes 6291460
  1.8 12.2 %all-to-all-start = ((bf16[8,32,256]{2,1,0:T(8,128)(2,1)}), bf16[8,32,256]{2,1,0:T(8,128)(2,1)S(1)}, u32[]{:S(2)}, u32[]{:S(2)}) async-start(bf16[8,32,256]{2,1,0:T(8,128)(2,1)} %shard_map.73), calls=%async_computation | async-start | bytes 262144 | tf_op jit(solution)/shard_map/all_to_all | solution.py:253
  9.7 4.3 %copy-start.1 = (bf16[2,2,256,128]{3,2,1,0:T(8,128)(2,1)S(1)}, bf16[2,2,256,128]{3,2,1,0:T(8,128)(2,1)}, u32[]{:S(2)}) copy-start(bf16[2,2,256,128]{3,2,1,0:T(8,128)(2,1)} %k_ref.3) | copy-start | bytes 786436
  9.7 4.3 %copy-start.2 = (bf16[2,2,256,128]{3,2,1,0:T(8,128)(2,1)S(1)}, bf16[2,2,256,128]{3,2,1,0:T(8,128)(2,1)}, u32[]{:S(2)}) copy-start(bf16[2,2,256,128]{3,2,1,0:T(8,128)(2,1)} %v_ref.1) | copy-start | bytes 786436
  15.2 9.5 %all-to-all-start.1 = ((f32[8,40,128]{2,1,0:T(8,128)}), f32[8,40,128]{2,1,0:T(8,128)S(1)}, u32[]{:S(2)}, u32[]{:S(2)}) async-start(f32[8,40,128]{2,1,0:T(8,128)} %shard_map.75), calls=%async_computation.1 | async-start | bytes 327680 | tf_op jit(solution)/shard_map/all_to_all | solution.py:253
  20.1 4.7 %collective-permute-start = (f32[40,128]{1,0:T(8,128)S(1)}, f32[40,128]{1,0:T(8,128)S(1)}, u32[]{:S(2)}, u32[]{:S(2)}) collective-permute-start(f32[40,128]{1,0:T(8,128)S(1)} %get-tuple-element.14), channel_id=1, source_target_pairs={{0,1},{1,0},{2,3},{3,2},{4,5},{5,4},{6,7},{7,6},{8,9},{9,8},{10,11... | collective-permute-start | bytes 61448 | tf_op jit(solution)/shard_map/ppermute | solution.py:321
  20.1 4.7 %collective-permute-start.1 = (f32[40,128]{1,0:T(8,128)S(1)}, f32[40,128]{1,0:T(8,128)S(1)}, u32[]{:S(2)}, u32[]{:S(2)}) collective-permute-start(f32[40,128]{1,0:T(8,128)S(1)} %get-tuple-element.15), channel_id=1, source_target_pairs={{0,2},{1,3},{2,0},{3,1},{4,6},{5,7},{6,4},{7,5},{8,10},{9,11},{10,... | collective-permute-start | bytes 61448 | tf_op jit(solution)/shard_map/ppermute | solution.py:321
  21.6 3.2 %collective-permute-start.2 = (f32[40,128]{1,0:T(8,128)S(1)}, f32[40,128]{1,0:T(8,128)S(1)}, u32[]{:S(2)}, u32[]{:S(2)}) collective-permute-start(f32[40,128]{1,0:T(8,128)S(1)} %get-tuple-element.16), channel_id=1, source_target_pairs={{0,3},{1,2},{2,1},{3,0},{4,7},{5,6},{6,5},{7,4},{8,11},{9,10},{10,... | collective-permute-start | bytes 61448 | tf_op jit(solution)/shard_map/ppermute | solution.py:321
